TPU v7x, 32 devices: a whole 2x2x4 slice. The times are simulated.
32 devices in a mesh: seq: 16 (over z, y, core), dp: 2 (over x).
Axes of the slice: x: 2, y: 2, z: 4, core: 2. Of those that a mesh axis runs over, the one named last changes fastest.
Arguments:
- acceptors: bfloat16 [2, 2048, 2560], P('dp', 'seq'), may hold values from -2 to 2
- lookups: bfloat16 [2, 2048, 2560], P('dp', 'seq'), may hold values from -0.625 to 0.625
- payloads: bfloat16 [2, 2048, 2560], P('dp', 'seq'), may hold values from -6 to 6
- lagged_fading_source: bfloat16 [2, 2048, 2560], P('dp', 'seq'), may hold values from -6 to 6
- response_cotangent: bfloat16 [2, 2048, 2560], P('dp', 'seq'), may hold values from -5 to 5
- fading_lowering_array: bfloat16 [2560, 128], replicated, may hold values from -0.125 to 0.125
- fading_raising_array: bfloat16 [2560, 128], replicated, may hold values from -1.25 to 1.25
- feature_fading_speed: float32 [2560], replicated, may hold values from 2.3251488e-05 to 0.125
- present_reward: float32 [2560], replicated, may hold values from 1.4142135 to 11.313708
Outputs:
- mixed: bfloat16 [2, 2048, 2560], P('dp', 'seq')
- grad_receptance: bfloat16 [2, 2048, 2560], P('dp', 'seq')
- lookup_deriv: bfloat16 [2, 2048, 2560], P('dp', 'seq')
- payload_deriv: bfloat16 [2, 2048, 2560], P('dp', 'seq')
- grad_decay_input: bfloat16 [2, 2048, 2560], P('dp', 'seq')
- grad_lora_a: float32 [2560, 128], P('dp')
- grad_lora_b: float32 [2560, 128], P('dp')
- grad_time_decay: float32 [2560], P('dp')
- present_reward_deriv: float32 [2560], P('dp')
All inputs are finite; a program needn't handle non-finite values.
Results may differ from a plain program's by a relative error of at most 0.006.
Values sent between devices are 32-bit elements.
A program may use at most 320 MiB of HBM per device.

v0:
```python
import jax
import jax.numpy as jnp
from jax import lax
from jax.sharding import PartitionSpec as P

ATTENDER_TOTAL = 40
LANE_TOTAL = 64
BLOCK = 64
HIGH = lax.Precision.HIGHEST


def carried_in(part, axis, combine, identity, reverse):
    count = lax.axis_size(axis)
    place = lax.axis_index(axis)
    ahead = count - 1 - place if reverse else place
    gathered = jax.tree.map(lambda a: lax.all_gather(a, axis), part)
    state = jax.tree.map(lambda a, e: jnp.zeros_like(a) + jnp.asarray(e, a.dtype), part, identity)

    def one(hop, state):
        source = count - 1 - hop if reverse else hop
        return combine(
            state, jax.tree.map(lambda a: lax.dynamic_index_in_dim(a, source, 0, False), gathered)
        )

    return lax.fori_loop(0, ahead, one, state)


def contract(pattern, left, right):
    return jnp.einsum(pattern, left, right, precision=HIGH, preferred_element_type=jnp.float32)


def decay_log_values(input_rows, fading_lowering_array, fading_raising_array, feature_fading_speed):
    apply_projection = jnp.dot(
        input_rows, fading_lowering_array, preferred_element_type=jnp.float32
    )
    smoothed_values = jnp.tanh(apply_projection)
    gate_portion = smoothed_values.astype(jnp.bfloat16)
    rank_projection = lax.dot_general(
        gate_portion,
        fading_raising_array,
        (((1,), (1,)), ((), ())),
        preferred_element_type=jnp.float32,
    )
    return (
        smoothed_values,
        gate_portion,
        -feature_fading_speed[None, :] * jnp.exp(rank_projection),
    )


def compose(decays, own_states, backward):

    def advance(carry, member):
        run_decay, run_state = carry
        decay, own_state = member
        return ((run_decay * decay, decay[..., None] * run_state + own_state), carry)

    initial = (
        jnp.ones(decays.shape[1:], jnp.float32),
        jnp.zeros(own_states.shape[1:], jnp.float32),
    )
    return lax.scan(advance, initial, (decays, own_states), reverse=backward)


def follow(earlier, later):
    return (earlier[0] * later[0], later[0][..., None] * earlier[1] + later[1])


def temporal_blend_sublevel(
    acceptor_lines,
    lookups,
    payloads,
    incoming_cotangent,
    fading_exponent,
    reward_by_attender,
    adjacent_shardlink,
):
    inclusive = jnp.cumsum(fading_exponent, axis=1)
    exclusive = inclusive - fading_exponent
    middle = inclusive[:, BLOCK // 2 - 1 : BLOCK // 2]
    overall = inclusive[:, -1]
    entering = jnp.exp(exclusive)
    leaving = jnp.exp(overall[:, None] - inclusive)
    upward = jnp.exp(exclusive - middle)
    downward = jnp.exp(middle - inclusive)
    decays = jnp.exp(overall)
    reached = acceptor_lines * entering
    faded_keys = lookups * leaving
    own_states = contract("nchk,nchv->nhkv", faded_keys, payloads)
    pull_states = contract("nchk,nchv->nhkv", reached, incoming_cotangent)
    starts, block_ends = adjacent_shardlink(decays, own_states, pull_states)
    position = jnp.arange(BLOCK)
    beneath = position[:, None] > position[None, :]
    early_recept = acceptor_lines * upward
    late_keys = lookups * downward
    scores = jnp.where(beneath, contract("nthk,nshk->nhts", early_recept, late_keys), 0.0)
    present_contribution = jnp.sum(acceptor_lines * reward_by_attender * lookups, axis=-1)[
        ..., None
    ]
    blended_response = (
        contract("nhts,nshv->nthv", scores, payloads)
        + present_contribution * payloads
        + contract("nthk,nhkv->nthv", reached, starts)
    )
    grad_start = decays[..., None] * block_ends + pull_states
    products = jnp.where(beneath, contract("nthv,nshv->nhts", incoming_cotangent, payloads), 0.0)
    agreement_verify = jnp.sum(payloads * incoming_cotangent, axis=-1)[..., None]
    memory_acceptors = entering * contract(
        "nhkv,nthv->nthk", starts, incoming_cotangent
    ) + upward * contract("nhts,nshk->nthk", products, late_keys)
    memory_lookup_lines = leaving * contract(
        "nhkv,nthv->nthk", block_ends, payloads
    ) + downward * contract("nhst,nshk->nthk", products, early_recept)
    payload_deriv = (
        contract("nthk,nhkv->nthv", faded_keys, block_ends)
        + contract("nhst,nshv->nthv", scores, incoming_cotangent)
        + present_contribution * incoming_cotangent
    )
    acceptor_deriv = memory_acceptors + reward_by_attender * lookups * agreement_verify
    lookup_deriv = memory_lookup_lines + reward_by_attender * acceptor_lines * agreement_verify
    present_reward_deriv = jnp.sum(acceptor_lines * lookups * agreement_verify, axis=(0, 1))
    coupling = jnp.sum(grad_start * starts, axis=-1)
    change = lookups * memory_lookup_lines - acceptor_lines * memory_acceptors
    fading_deriv = (
        coupling[:, None] + jnp.cumsum(change, axis=1) - change - acceptor_lines * memory_acceptors
    )
    return (
        blended_response,
        acceptor_deriv,
        lookup_deriv,
        payload_deriv,
        fading_deriv,
        present_reward_deriv,
    )


def sublevel_evaluation(
    reshaped_acceptors,
    reshaped_lookups,
    reshaped_payloads,
    reshaped_source,
    incoming_cotangent_reshaped,
    fading_lowering_array,
    fading_raising_array,
    feature_fading_speed,
    present_reward,
    adjacent_shardlink,
):
    smoothed_values, gate_portion, fading_exponent = decay_log_values(
        reshaped_source, fading_lowering_array, fading_raising_array, feature_fading_speed
    )
    tokens, feature_span = reshaped_acceptors.shape
    tiling_arrangement = (tokens // BLOCK, BLOCK, ATTENDER_TOTAL, LANE_TOTAL)
    collected_outcomes = temporal_blend_sublevel(
        reshaped_acceptors.astype(jnp.float32).reshape(tiling_arrangement),
        reshaped_lookups.astype(jnp.float32).reshape(tiling_arrangement),
        reshaped_payloads.astype(jnp.float32).reshape(tiling_arrangement),
        incoming_cotangent_reshaped.astype(jnp.float32).reshape(tiling_arrangement),
        fading_exponent.reshape(tiling_arrangement),
        present_reward.reshape(ATTENDER_TOTAL, LANE_TOTAL),
        adjacent_shardlink,
    )
    (
        blended_response,
        acceptor_deriv,
        lookup_deriv,
        payload_deriv,
        fading_deriv,
        present_reward_deriv,
    ) = collected_outcomes
    slope = fading_deriv.reshape(tokens, feature_span) * fading_exponent
    slope_portion = slope.astype(jnp.bfloat16)
    gate_gradient = jnp.dot(slope_portion, fading_raising_array, preferred_element_type=jnp.float32)
    projection_gradient = (gate_gradient * (1.0 - smoothed_values * smoothed_values)).astype(
        jnp.bfloat16
    )
    input_gradient = lax.dot_general(
        projection_gradient,
        fading_lowering_array,
        (((1,), (1,)), ((), ())),
        preferred_element_type=jnp.float32,
    ).astype(jnp.bfloat16)
    lowering_array_deriv = lax.dot_general(
        reshaped_source,
        projection_gradient,
        (((0,), (0,)), ((), ())),
        preferred_element_type=jnp.float32,
    )
    raising_array_deriv = lax.dot_general(
        slope_portion, gate_portion, (((0,), (0,)), ((), ())), preferred_element_type=jnp.float32
    )
    speed_deriv = jnp.sum(slope, axis=0)

    def flatten(member):
        return member.reshape(tokens, feature_span).astype(jnp.bfloat16)

    return (
        flatten(blended_response),
        flatten(acceptor_deriv),
        flatten(lookup_deriv),
        flatten(payload_deriv),
        input_gradient,
        (
            lowering_array_deriv,
            raising_array_deriv,
            speed_deriv,
            present_reward_deriv.reshape(feature_span),
        ),
    )


def shard_link(decays, own_states, pull_states):
    ahead_total, ahead = compose(decays, own_states, False)
    behind_total, behind = compose(decays, pull_states, True)
    identity = (jnp.ones_like(ahead_total[0]), jnp.zeros_like(ahead_total[1]))
    prior, state_in = carried_in(ahead_total, "seq", follow, identity, False)
    latter, grad_after = carried_in(behind_total, "seq", follow, identity, True)
    starts = ahead[0][..., None] * state_in[None] + ahead[1]
    block_ends = behind[0][..., None] * grad_after[None] + behind[1]
    return (starts, block_ends)


def per_device(
    acceptors,
    lookups,
    payloads,
    lagged_fading_source,
    response_cotangent,
    fading_lowering_array,
    fading_raising_array,
    feature_fading_speed,
    present_reward,
):
    collected_outcomes = sublevel_evaluation(
        acceptors[0],
        lookups[0],
        payloads[0],
        lagged_fading_source[0],
        response_cotangent[0],
        fading_lowering_array,
        fading_raising_array,
        feature_fading_speed,
        present_reward,
        shard_link,
    )
    sums = collected_outcomes[5]
    dp_count = lax.axis_size("dp")
    share_rows = fading_lowering_array.shape[0] // dp_count
    whole = lax.psum((sums[0], sums[1], sums[2], sums[3]), ("seq", "dp"))
    offset = lax.axis_index("dp") * share_rows
    reduced = tuple((lax.dynamic_slice_in_dim(member, offset, share_rows, 0) for member in whole))
    return (
        collected_outcomes[0][None],
        collected_outcomes[1][None],
        collected_outcomes[2][None],
        collected_outcomes[3][None],
        collected_outcomes[4][None],
        reduced[0],
        reduced[1],
        reduced[2],
        reduced[3],
    )


def solution(mesh):
    in_specs = (
        P("dp", "seq", None),
        P("dp", "seq", None),
        P("dp", "seq", None),
        P("dp", "seq", None),
        P("dp", "seq", None),
        P(),
        P(),
        P(),
        P(),
    )
    out_specs = (
        P("dp", "seq", None),
        P("dp", "seq", None),
        P("dp", "seq", None),
        P("dp", "seq", None),
        P("dp", "seq", None),
        P("dp", None),
        P("dp", None),
        P("dp"),
        P("dp"),
    )
    return jax.shard_map(
        per_device, mesh=mesh, in_specs=in_specs, out_specs=out_specs, check_vma=False
    )
```

profile of v0, /device:TPU:0, one launch (start us, length us, event | category | flops | bytes accessed | tf_op | source)
XLA Modules:
  0.0 555.1 jit_solution(3904437213683768561)
XLA Ops:
  19.8 2.9 reshape.128
  22.7 3.2 copy.93
  28.6 5.5 fusion.57
  36.0 17.7 %while.66 = (s32[]{:T(128)}, f32[40,64]{1,0:T(8,128)S(1)}, f32[40,64,64]{2,1,0:T(8,128)}, f32[2,40,64]{2,1,0:T(8,128)S(1)}, f32[2,40,64,64]{2,3,1,0:T(8,128)}, /...) while((s32[]{:T(128)}, f32[40,64]{1,0:T(8,128)S(1)}, ...), condition=%wide.region_3.4_spmd.clone, body=%wide.region_2.3_spmd.clone.sunk | while | flops 499203 | bytes 6646389 | solution.py:62
  36.0 3.2 select_bitcast_fusion.4
  39.3 2.8 copy.180
  44.6 3.6 select_bitcast_fusion.4
  48.3 2.8 copy.180
  53.9 3.3 copy.90
  59.8 2.8 reshape.127
  62.6 3.6 copy.91
  66.2 7.1 %fusion.50 = f32[2,40,64,64]{2,3,1,0:T(8,128)} fusion(f32[2,64,40,64]{1,3,2,0:T(8,128)} %copy.91, bf16[2,64,40,64]{3,2,1,0:T(8,128)(2,1)} %reshape.125, f32[2,64,40,64]{1,3,2,0:T(8,128)S(1)} %copy.89, f32[2,64,40,64]{1,3,2,0:T(8,128)} %copy.90), kind=kOutput, calls=%fused_computation.85 | convolution fusion | flops 252313600 | bytes 5898240 | tf_op jit(solution)/shard_map/nchk,nchv->nhkv/dot_general | solution.py:29
  75.7 29.7 %while.67 = (s32[]{:T(128)}, f32[40,64]{1,0:T(8,128)S(1)}, f32[40,64,64]{2,1,0:T(8,128)}, f32[2,40,64]{2,1,0:T(8,128)}, f32[2,40,64,64]{2,3,1,0:T(8,128)}, /*ind...) while((s32[]{:T(128)}, f32[40,64]{1,0:T(8,128)S(1)}, ...), condition=%wide.region_8.9_spmd.clone, body=%wide.region_7.8_spmd.clone.sunk | while | flops 499204 | bytes 9257093 | solution.py:62
  76.3 2.7 constant_dynamic-slice_fusion.4
  79.0 2.8 copy.181
  81.8 3.3 select_bitcast_fusion.5
  85.0 2.8 copy.182
  93.6 2.8 copy.181
  96.4 3.7 select_bitcast_fusion.5
  100.1 2.8 copy.182
  106.3 3.1 fusion.5
  110.8 2.7 mul.266.clone
  113.5 2.9 mul.285
  116.3 27.7 %all-gather = f32[640,64]{1,0:T(8,128)} all-gather(f32[40,64]{1,0:T(8,128)S(1)} %get-tuple-element.322), channel_id=2, replica_groups=mesh['seq'=16,'dp'=2] {'seq'}, dimensions={0}, use_global_device_ids=true | all-gather | bytes 174080 | tf_op jit(solution)/shard_map/all_gather | solution.py:16
  144.0 21.9 %all-gather.2 = f32[640,64]{1,0:T(8,128)} all-gather(f32[40,64]{1,0:T(8,128)S(1)} %get-tuple-element.327), channel_id=4, replica_groups=mesh['seq'=16,'dp'=2] {'seq'}, dimensions={0}, use_global_device_ids=true | all-gather | bytes 174080 | tf_op jit(solution)/shard_map/all_gather | solution.py:16
  166.0 2.8 multiply_reduce_fusion.2
  168.8 4.1 fusion.62
  172.9 7.7 %fusion.52 = f32[2,40,64,64]{3,2,1,0:T(8,128)} fusion(f32[2,64,40,64]{1,3,2,0:T(8,128)S(1)} %copy-done.3, f32[2,64,40,64]{1,3,2,0:T(8,128)S(1)} %copy.89, f32[2,40,64]{2,1,0:T(8,128)S(1)} %get-tuple-element.494, f32[2,64,40,64]{1,3,2,0:T(8,128)S(1)} %copy-done.6, f32[2,64,40,64]{1,3,2,0:T(8,128)S(1)} %copy-done.1), kind=kOutput, calls=%fused_computation.86 | convolution fusion | flops 253296640 | bytes 6574080 | tf_op jit(solution)/shard_map/nthk,nshk->nhts/dot_general | solution.py:29
  182.0 2.8 copy.103
  184.8 97.0 %all-gather.9.cloned.1.call-done = f32[640,64,64]{2,1,0:T(8,128)} async-done(((f32[40,64,64]{2,1,0:T(8,128)}), f32[640,64,64]{2,1,0:T(8,128)}) %all-gather.9.cloned.1.call-update) | async-done | bytes 10485776 | tf_op jit(solution)/shard_map/all_gather | solution.py:16
  283.1 60.2 %while.65 = (s32[]{:T(128)}, f32[40,64,64]{2,1,0:T(8,128)}, s32[]{:T(128)}, f32[16,40,64]{2,1,0:T(8,128)}, f32[16,40,64,64]{3,2,1,0:T(8,128)}, /*index=5*/s32[]{:T(128)}, s32[]{:T(128)}, s32[]{:T(128)}, s32[]{:T(128)}) while((s32[]{:T(128)}, f32[40,64,64]{2,1,0:T(8,128)}, s32[]{:T(128)}, f32[16,40,64]{2,1,0:T(8,128)}, ...), condition=%wide.region_10.11_spmd, body=%wide.region_9.10_spmd.sunk | while | flops 327686 | bytes 1996947 | solution.py:25
  283.8 3.3 bitcast_add_fusion.8
  287.8 3.3 bitcast_add_fusion.8
  291.8 3.3 bitcast_add_fusion.8
  295.8 3.3 bitcast_add_fusion.8
  299.8 3.3 bitcast_add_fusion.8
  303.9 3.3 bitcast_add_fusion.8
  307.9 3.3 bitcast_add_fusion.8
  311.9 3.3 bitcast_add_fusion.8
  315.9 3.3 bitcast_add_fusion.8
  319.9 3.3 bitcast_add_fusion.8
  323.9 3.3 bitcast_add_fusion.8
  327.9 3.3 bitcast_add_fusion.8
  331.9 3.3 bitcast_add_fusion.8
  335.9 3.3 bitcast_add_fusion.8
  339.9 3.3 bitcast_add_fusion.8
  343.2 2.8 copy.119
  346.1 6.4 %fusion.24 = f32[2,40,64,64]{3,2,1,0:T(8,128)} fusion(f32[2,40,64,64]{2,3,1,0:T(8,128)} %get-tuple-element.330, f32[40,64,64]{1,2,0:T(8,128)} %copy.119, f32[2,40,64]{2,1,0:T(8,128)S(1)} %copy-done.23, bf16[2,64,40,64]{3,2,1,0:T(8,128)(2,1)} %reshape.124), kind=kOutput, calls=%fused_computation.64 | convolution fusion | flops 252313600 | bytes 3952640 | tf_op jit(solution)/shard_map/nhkv,nthv->nthk/dot_general | solution.py:29
  352.5 4.1 multiply_reduce_fusion
  359.9 6.5 %fusion.9 = f32[2,64,40,64]{1,3,2,0:T(8,128)} fusion(f32[2,40,64,64]{3,2,1,0:T(8,128)S(1)} %fusion.21, f32[2,40,64,64]{3,2,1,0:T(8,128)S(1)} %copy-done.16, f32[2,40,64]{2,1,0:T(8,128)S(1)} %get-tuple-element.494, pred[64,64]{1,0:T(8,128)(4,1)S(1)} %iota_compare_fusion, f32[2,64,40,64]{1,3,2,0:T(8,128)S(1)} %copy-done.4, f32[2,64,40,64]{1,3,2,0:T(8,128)S(1)} %copy.89, ...), kind=kOutput, calls=%fused_computation.36 | convolution fusion | flops 254279680 | bytes 7888896 | tf_op jit(solution)/shard_map/nhts,nshk->nthk/dot_general | solution.py:29
  366.4 11.1 %multiply_subtract_fusion = (f32[2,64,40,64]{1,3,2,0:T(8,128)}, f32[2,64,40,64]{1,3,2,0:T(8,128)}, bf16[2,64,40,64]{1,3,2,0:T(8,128)(2,1)}, bf16[2,64,40,64]{1,3,2,0:T(8,128)(2,1)}, f32[2,64,40]{1,2,0:T(8,128)}) fusion(f32[2,64,40,64]{1,3,2,0:T(8,128)S(1)} %copy-done.4, f32[2,64,40,64]{1,3,2,0:T(8,128)S(1)} %copy-done.7, f32[2,64,40,64]{1,3,2,0:T(8,128)} %fusion.9, ...), kind=kOutput, calls=%fused_computation.39 | convolution fusion | flops 258862080 | bytes 13203456 | tf_op jit(solution)/shard_map/nhst,nshk->nthk/dot_general | solution.py:29
  377.5 3.2 copy.131
  380.7 3.5 fusion.83
  384.2 3.2 copy.132
  387.4 5.0 subtract_subtract_fusion
  392.4 3.3 copy.133
  395.7 3.2 reshape.126
  403.0 6.6 %fusion.23 = f32[2,40,64,64]{2,3,1,0:T(8,128)} fusion(f32[2,40,64,64]{2,3,1,0:T(8,128)S(1)} %copy-done.13, f32[40,64,64]{1,2,0:T(8,128)S(1)} %copy-done.18, f32[2,40,64]{2,1,0:T(8,128)S(1)} %copy-done.24, f32[2,64,40,64]{1,3,2,0:T(8,128)S(1)} %copy-done.5, f32[2,64,40,64]{1,3,2,0:T(8,128)S(1)} %copy.89, f32[2,40,64]{2,1,0:T(8,128)S(1)} %copy-done.22), kind=kOutput, calls=%fused_computation.63 | convolution fusion | flops 252968960 | bytes 5939200 | tf_op jit(solution)/shard_map/nthk,nhkv->nthv/dot_general | solution.py:29
  411.1 7.4 %fusion.7 = bf16[2,64,40,64]{3,1,2,0:T(8,128)(2,1)} fusion(f32[2,40,64,64]{2,3,1,0:T(8,128)} %fusion.23, f32[2,40,64,64]{3,2,1,0:T(8,128)} %fusion.52, f32[2,64,40]{1,2,0:T(8,128)S(1)} %copy-done.26, pred[64,64]{1,0:T(8,128)(4,1)S(1)} %iota_compare_fusion, bf16[2,64,40,64]{3,2,1,0:T(8,128)(2,1)} %reshape.125), kind=kOutput, calls=%fused_computation.30 | convolution fusion | flops 253624320 | bytes 3956736 | tf_op jit(solution)/shard_map/nhst,nshv->nthv/dot_general | solution.py:29
  418.6 37.4 %all-reduce = (f32[2560]{0:T(1024)S(1)}, f32[2560]{0:T(1024)S(1)}) all-reduce(f32[2560]{0:T(1024)S(1)} %get-tuple-element.492, f32[2560]{0:T(1024)S(1)} %copy-done.29), channel_id=1, replica_groups=mesh['seq'=16,'dp'=2] {'seq','dp'}, use_global_device_ids=true, to_apply=%region_16.17 | all-reduce | flops 5120 | bytes 40960 | tf_op jit(solution)/shard_map/psum | solution.py:249
  457.3 3.2 copy.128
  460.6 2.8 convert_element_type.122
  463.3 8.7 %fusion.22 = f32[2,40,64,64]{2,3,1,0:T(8,128)S(1)} fusion(f32[2,40,64,64]{2,3,1,0:T(8,128)} %get-tuple-element.325, f32[40,64,64]{1,2,0:T(8,128)} %copy.103, f32[2,40,64]{2,1,0:T(8,128)S(1)} %get-tuple-element.321, f32[2,64,40,64]{1,3,2,0:T(8,128)} %copy.91, f32[2,64,40,64]{1,3,2,0:T(8,128)S(1)} %copy.89, f32[2,64,40,64]{1,3,2,0:T(8,128)} %copy.90), kind=kOutput, calls=%fused_computation.62 | convolution fusion | flops 252968960 | bytes 7229440 | tf_op jit(solution)/shard_map/nthk,nhkv->nthv/dot_general | solution.py:29
  485.3 59.9 %all-reduce.4.cloned.1.call-done = (f32[2560,128]{0,1:T(8,128)}, f32[2560,128]{1,0:T(8,128)}) async-done(((f32[2560,128]{0,1:T(8,128)}, f32[2560,128]{1,0:T(8,128)}), (f32[2560,128]{0,1:T(8,128)}, f32[2560,128]{1,0:T(8,128)})) %all-reduce.4.cloned.1.call-update) | async-done | bytes 2621456 | tf_op jit(solution)/shard_map/psum | solution.py:249
  (137 shorter events, 78.9 us)
Async XLA Ops:
  7.2 2.4 copy-start
  7.2 173.4 %all-gather.7.cloned.1.call-start = ((), (), s32[]{:S(2)}) async-start(), calls=%async_computation | async-start | bytes 22282240 | tf_op jit(solution)/shard_map/all_gather | solution.py:16
  12.8 1.5 copy-start.14
  18.9 9.7 %copy-start.21 = (f32[2,40,64]{2,1,0:T(8,128)}, f32[2,40,64]{2,1,0:T(8,128)S(1)}, u32[]{:S(2)}) copy-start(f32[2,40,64]{2,1,0:T(8,128)S(1)} %get-tuple-element.495) | copy-start | bytes 61444
  53.7 228.2 %all-gather.9.cloned.1.call-start = ((), (), s32[]{:S(2)}) async-start(), calls=%async_computation.1 | async-start | bytes 22282240 | tf_op jit(solution)/shard_map/all_gather | solution.py:16
  105.4 439.8 %all-reduce.4.cloned.1.call-start = ((), (), s32[]{:S(2)}) async-start(), calls=%async_computation.2 | async-start | bytes 5242880 | tf_op jit(solution)/shard_map/psum | solution.py:249
  166.0 6.9 %copy-start.6 = (f32[2,64,40,64]{1,3,2,0:T(8,128)S(1)}, f32[2,64,40,64]{1,3,2,0:T(8,128)}, u32[]{:S(2)}) copy-start(f32[2,64,40,64]{1,3,2,0:T(8,128)} %copy.91) | copy-start | bytes 3932164
  168.8 4.1 copy-start.1
  168.8 4.1 copy-start.3
  343.2 2.8 copy-start.23
  346.0 6.4 %copy-start.8 = (f32[2,40,64,64]{2,3,1,0:T(8,128)S(1)}, f32[2,40,64,64]{2,3,1,0:T(8,128)}, u32[]{:S(2)}) copy-start(f32[2,40,64,64]{2,3,1,0:T(8,128)} %get-tuple-element.773) | copy-start | bytes 3932164
  346.0 6.4 %copy-start.11 = (f32[2,40,64,64]{2,3,1,0:T(8,128)S(1)}, f32[2,40,64,64]{2,3,1,0:T(8,128)}, u32[]{:S(2)}) copy-start(f32[2,40,64,64]{2,3,1,0:T(8,128)} %get-tuple-element.325) | copy-start | bytes 3932164
  346.0 6.4 %copy-start.12 = (f32[2,40,64,64]{2,3,1,0:T(8,128)S(1)}, f32[2,40,64,64]{2,3,1,0:T(8,128)}, u32[]{:S(2)}) copy-start(f32[2,40,64,64]{2,3,1,0:T(8,128)} %get-tuple-element.330) | copy-start | bytes 3932164
  352.5 4.1 copy-start.10
  352.5 4.1 copy-start.17
  356.6 2.4 copy-start.2
  356.6 2.5 copy-start.4
  356.6 3.3 copy-start.16
  359.9 6.5 %copy-start.7 = (f32[2,64,40,64]{1,3,2,0:T(8,128)S(1)}, f32[2,64,40,64]{1,3,2,0:T(8,128)}, u32[]{:S(2)}) copy-start(f32[2,64,40,64]{1,3,2,0:T(8,128)} %copy.91) | copy-start | bytes 3932164
  359.9 6.5 %copy-start.22 = (f32[2,40,64]{2,1,0:T(8,128)S(1)}, f32[2,40,64]{2,1,0:T(8,128)}, u32[]{:S(2)}) copy-start(f32[2,40,64]{2,1,0:T(8,128)} %copy-done.21) | copy-start | bytes 61444
  359.9 6.5 %copy-start.25 = (f32[2,64,40]{1,2,0:T(8,128)S(1)}, f32[2,64,40]{1,2,0:T(8,128)}, u32[]{:S(2)}) copy-start(f32[2,64,40]{1,2,0:T(8,128)} %fusion.5) | copy-start | bytes 61444
  384.2 3.2 copy-start.28
  398.9 3.9 copy-start.5
  398.9 3.9 copy-start.13
  398.9 4.1 copy-start.18
  398.9 4.1 copy-start.24
  403.0 6.6 %copy-start.20 = (bf16[1,128,2560]{2,1,0:T(8,128)(2,1)S(1)}, bf16[1,128,2560]{2,1,0:T(8,128)(2,1)}, u32[]{:S(2)}) copy-start(bf16[1,128,2560]{2,1,0:T(8,128)(2,1)} %param.20) | copy-start | bytes 1966084
  409.7 1.4 copy-start.26
  411.1 7.5 %copy-start.29 = (f32[2560]{0:T(1024)S(1)}, f32[2560]{0:T(1024)}, u32[]{:S(2)}) copy-start(f32[2560]{0:T(1024)} %multiply_reduce_fusion.2) | copy-start | bytes 30724
  463.3 8.7 %copy-start.9 = (bf16[2,64,40,64]{3,2,1,0:T(8,128)(2,1)S(1)}, bf16[2,64,40,64]{3,2,1,0:T(8,128)(2,1)}, u32[]{:S(2)}) copy-start(bf16[2,64,40,64]{3,2,1,0:T(8,128)(2,1)} %reshape.124) | copy-start | bytes 1966084
  463.3 8.7 %copy-start.15 = (f32[2,40,64,64]{3,2,1,0:T(8,128)S(1)}, f32[2,40,64,64]{3,2,1,0:T(8,128)}, u32[]{:S(2)}) copy-start(f32[2,40,64,64]{3,2,1,0:T(8,128)} %fusion.52) | copy-start | bytes 3932164
  476.9 3.6 copy-start.19
  545.2 2.3 copy-start.27
Sparse Core Ops, SparseCore 0:
  53.8 117.4 all-gather.6
  172.8 108.9 all-gather.8
  411.2 133.9 all-reduce.3
where the time goes:
time: 564 us; the launch traced here: 555 us
  waiting for transfers between devices  157 us (28%)
  local copies, waits for them, and re-layouts  125 us (22%)
  other arithmetic  87.2 us (15%)
  blocking collectives  87 us (15%)
  matrix products  84.5 us (15%)
  between operations  14.3 us (3%)
    all_gather x2, waiting for transfers between devices, carried_in(): gathered = jax.tree.map(lambda a: lax.all_gather(a, axis), part)  97 us
    dot_general x12, matrix products, contract(): jnp.einsum(pattern, left, right, precision=HIGH, preferred_element_type=j...  76 us
    psum x1, waiting for transfers between devices, per_device(): whole = lax.psum((sums[0], sums[1], sums[2], sums[3]), ('seq', 'dp'))  59.9 us
    all_gather x2, blocking collectives, carried_in(): gathered = jax.tree.map(lambda a: lax.all_gather(a, axis), part)  49.6 us
    add x15, other arithmetic, follow(): return (earlier[0] * later[0], later[0][..., None] * earlier[1] + later[1])  49.2 us
    psum x1, blocking collectives, per_device(): whole = lax.psum((sums[0], sums[1], sums[2], sums[3]), ('seq', 'dp'))  37.4 us
    dynamic_update_slice x8, local copies, waits for them, and re-layouts, compose(): return lax.scan(advance, initial, (decays, own_states), reverse=backward)  21.4 us
    convert_element_type x8, local copies, waits for them, and re-layouts, flatten(): return member.reshape(tokens, feature_span).astype(jnp.bfloat16)  14.5 us
  transfers between devices with their start and end apart: 3, of which 2 were waited for; matrix products, arithmetic and copies ran while one was open for 21% of the time, Pallas kernels for 0%

commit v1 on v0

--- a/solution.py
+++ b/solution.py
@@ -1,3 +1,4 @@
+import functools
 import jax
 import jax.numpy as jnp
 from jax import lax
@@ -7,6 +8,14 @@
 LANE_TOTAL = 64
 BLOCK = 64
 HIGH = lax.Precision.HIGHEST
+
+
+def _make_lines(sheet, group_axis, mesh_dim):
+    f_next = lax.psum(lax.psum(sheet, group_axis), mesh_dim)
+    return f_next
+
+
+direct_tasks = functools.partial(_make_lines, group_axis="dp", mesh_dim="seq")
 
 
 def carried_in(part, axis, combine, identity, reverse):
@@ -246,7 +255,7 @@
     sums = collected_outcomes[5]
     dp_count = lax.axis_size("dp")
     share_rows = fading_lowering_array.shape[0] // dp_count
-    whole = lax.psum((sums[0], sums[1], sums[2], sums[3]), ("seq", "dp"))
+    whole = direct_tasks((sums[0], sums[1], sums[2], sums[3]))
     offset = lax.axis_index("dp") * share_rows
     reduced = tuple((lax.dynamic_slice_in_dim(member, offset, share_rows, 0) for member in whole))
     return (

time: 564 us -> 599 us (1.062)
  blocking collectives: 87 us -> 117 us
  waiting for transfers between devices: 157 us -> 164 us
    psum x1 -> x2, blocking collectives: 37.4 us -> 67.6 us  [_make_lines(): f_next = lax.psum(lax.psum(sheet, group_axis), mesh_dim)]
    all_gather x2, waiting for transfers between devices: 97 us -> 116 us  [carried_in(): gathered = jax.tree.map(lambda a: lax.all_gather(a, axis), part)]
    psum x1 -> x2, waiting for transfers between devices: 59.9 us -> 47.4 us  [_make_lines(): f_next = lax.psum(lax.psum(sheet, group_axis), mesh_dim)]
  transfers between devices with their start and end apart: 3 -> 4, of which waited for: 2 -> 4; matrix products, arithmetic and copies ran while one was open for 21% -> 21% of each run, Pallas kernels for 0% -> 0%
where the time goes in v1:
time: 599 us; the launch traced here: 591 us
  waiting for transfers between devices  164 us (27%)
  local copies, waits for them, and re-layouts  124 us (21%)
  blocking collectives  117 us (20%)
  other arithmetic  86.2 us (14%)
  matrix products  84.8 us (14%)
  between operations  14.3 us (2%)
    all_gather x2, waiting for transfers between devices, carried_in(): gathered = jax.tree.map(lambda a: lax.all_gather(a, axis), part)  116 us
    dot_general x12, matrix products, contract(): jnp.einsum(pattern, left, right, precision=HIGH, preferred_element_type=j...  76.4 us
    psum x2, blocking collectives, _make_lines(): f_next = lax.psum(lax.psum(sheet, group_axis), mesh_dim)  67.6 us
    all_gather x2, blocking collectives, carried_in(): gathered = jax.tree.map(lambda a: lax.all_gather(a, axis), part)  49.7 us
    add x15, other arithmetic, follow(): return (earlier[0] * later[0], later[0][..., None] * earlier[1] + later[1])  49.2 us
    psum x2, waiting for transfers between devices, _make_lines(): f_next = lax.psum(lax.psum(sheet, group_axis), mesh_dim)  47.4 us
    dynamic_update_slice x8, local copies, waits for them, and re-layouts, compose(): return lax.scan(advance, initial, (decays, own_states), reverse=backward)  21.6 us
    convert_element_type x8, local copies, waits for them, and re-layouts, flatten(): return member.reshape(tokens, feature_span).astype(jnp.bfloat16)  14.6 us
  transfers between devices with their start and end apart: 4, of which 4 were waited for; matrix products, arithmetic and copies ran while one was open for 21% of the time, Pallas kernels for 0%

profile of v1, /device:TPU:0, one launch (start us, length us, event | category | flops | bytes accessed | tf_op | source)
XLA Modules:
  0.0 590.7 jit_solution(2860252752915887187)
XLA Ops:
  19.8 2.9 reshape.128
  22.7 3.2 copy.93
  28.6 5.5 fusion.57
  35.9 17.7 %while.66 = (s32[]{:T(128)}, f32[40,64]{1,0:T(8,128)S(1)}, f32[40,64,64]{2,1,0:T(8,128)}, f32[2,40,64]{2,1,0:T(8,128)S(1)}, f32[2,40,64,64]{2,3,1,0:T(8,128)}, /...) while((s32[]{:T(128)}, f32[40,64]{1,0:T(8,128)S(1)}, ...), condition=%wide.region_3.4_spmd.clone, body=%wide.region_2.3_spmd.clone.sunk | while | flops 499203 | bytes 6646389 | solution.py:71
  36.0 3.2 select_bitcast_fusion.4
  39.2 2.9 copy.180
  44.6 3.6 select_bitcast_fusion.4
  48.2 2.9 copy.180
  53.8 3.3 copy.90
  57.2 2.7 reshape.125
  59.8 2.8 reshape.127
  62.6 3.6 copy.91
  66.2 7.0 %fusion.50 = f32[2,40,64,64]{2,3,1,0:T(8,128)} fusion(f32[2,64,40,64]{1,3,2,0:T(8,128)} %copy.91, bf16[2,64,40,64]{3,2,1,0:T(8,128)(2,1)} %reshape.125, f32[2,64,40,64]{1,3,2,0:T(8,128)S(1)} %copy.89, f32[2,64,40,64]{1,3,2,0:T(8,128)} %copy.90), kind=kOutput, calls=%fused_computation.85 | convolution fusion | flops 252313600 | bytes 5898240 | tf_op jit(solution)/shard_map/nchk,nchv->nhkv/dot_general | solution.py:38
  75.6 29.7 %while.67 = (s32[]{:T(128)}, f32[40,64]{1,0:T(8,128)S(1)}, f32[40,64,64]{2,1,0:T(8,128)}, f32[2,40,64]{2,1,0:T(8,128)}, f32[2,40,64,64]{2,3,1,0:T(8,128)}, /*ind...) while((s32[]{:T(128)}, f32[40,64]{1,0:T(8,128)S(1)}, ...), condition=%wide.region_8.9_spmd.clone, body=%wide.region_7.8_spmd.clone.sunk | while | flops 499204 | bytes 9257093 | solution.py:71
  76.2 2.7 constant_dynamic-slice_fusion.4
  78.9 2.8 copy.181
  81.7 3.2 select_bitcast_fusion.5
  84.9 2.8 copy.182
  93.5 2.8 copy.181
  96.3 3.6 select_bitcast_fusion.5
  99.9 2.8 copy.182
  106.2 27.8 %all-gather = f32[640,64]{1,0:T(8,128)} all-gather(f32[40,64]{1,0:T(8,128)S(1)} %get-tuple-element.322), channel_id=2, replica_groups=mesh['seq'=16,'dp'=2] {'seq'}, dimensions={0}, use_global_device_ids=true | all-gather | bytes 174080 | tf_op jit(solution)/shard_map/all_gather | solution.py:25
  134.0 21.9 %all-gather.2 = f32[640,64]{1,0:T(8,128)} all-gather(f32[40,64]{1,0:T(8,128)S(1)} %get-tuple-element.327), channel_id=4, replica_groups=mesh['seq'=16,'dp'=2] {'seq'}, dimensions={0}, use_global_device_ids=true | all-gather | bytes 174080 | tf_op jit(solution)/shard_map/all_gather | solution.py:25
  155.9 3.2 fusion.5
  161.5 9.7 %all-gather.7.cloned.1.call-done = f32[640,64,64]{2,1,0:T(8,128)} async-done(((f32[40,64,64]{2,1,0:T(8,128)}), f32[640,64,64]{2,1,0:T(8,128)}) %all-gather.7.cloned.1.call-update) | async-done | bytes 10485776 | tf_op jit(solution)/shard_map/all_gather | solution.py:25
  172.4 2.8 copy.103
  175.2 106.6 %all-gather.9.cloned.1.call-done = f32[640,64,64]{2,1,0:T(8,128)} async-done(((f32[40,64,64]{2,1,0:T(8,128)}), f32[640,64,64]{2,1,0:T(8,128)}) %all-gather.9.cloned.1.call-update) | async-done | bytes 10485776 | tf_op jit(solution)/shard_map/all_gather | solution.py:25
  283.0 60.3 %while.65 = (s32[]{:T(128)}, f32[40,64,64]{2,1,0:T(8,128)}, s32[]{:T(128)}, f32[16,40,64]{2,1,0:T(8,128)}, f32[16,40,64,64]{3,2,1,0:T(8,128)}, /*index=5*/s32[]{:T(128)}, s32[]{:T(128)}, s32[]{:T(128)}, s32[]{:T(128)}) while((s32[]{:T(128)}, f32[40,64,64]{2,1,0:T(8,128)}, s32[]{:T(128)}, f32[16,40,64]{2,1,0:T(8,128)}, ...), condition=%wide.region_10.11_spmd, body=%wide.region_9.10_spmd.sunk | while | flops 327686 | bytes 1996947 | solution.py:34
  283.8 3.3 bitcast_add_fusion.8
  287.8 3.3 bitcast_add_fusion.8
  291.8 3.3 bitcast_add_fusion.8
  295.8 3.3 bitcast_add_fusion.8
  299.8 3.3 bitcast_add_fusion.8
  303.8 3.3 bitcast_add_fusion.8
  307.8 3.3 bitcast_add_fusion.8
  311.8 3.3 bitcast_add_fusion.8
  315.9 3.3 bitcast_add_fusion.8
  319.9 3.3 bitcast_add_fusion.8
  323.9 3.3 bitcast_add_fusion.8
  327.9 3.3 bitcast_add_fusion.8
  331.9 3.3 bitcast_add_fusion.8
  335.9 3.3 bitcast_add_fusion.8
  339.9 3.3 bitcast_add_fusion.8
  343.4 2.8 copy.119
  346.2 6.4 %fusion.24 = f32[2,40,64,64]{3,2,1,0:T(8,128)} fusion(f32[2,40,64,64]{2,3,1,0:T(8,128)} %get-tuple-element.330, f32[40,64,64]{1,2,0:T(8,128)} %copy.119, f32[2,40,64]{2,1,0:T(8,128)S(1)} %copy-done.23, bf16[2,64,40,64]{3,2,1,0:T(8,128)(2,1)} %reshape.124), kind=kOutput, calls=%fused_computation.64 | convolution fusion | flops 252313600 | bytes 3952640 | tf_op jit(solution)/shard_map/nhkv,nthv->nthk/dot_general | solution.py:38
  352.7 4.1 multiply_reduce_fusion
  360.1 6.7 %fusion.9 = f32[2,64,40,64]{1,3,2,0:T(8,128)} fusion(f32[2,40,64,64]{3,2,1,0:T(8,128)S(1)} %fusion.21, f32[2,40,64,64]{3,2,1,0:T(8,128)S(1)} %copy-done.16, f32[2,40,64]{2,1,0:T(8,128)S(1)} %get-tuple-element.498, pred[64,64]{1,0:T(8,128)(4,1)S(1)} %iota_compare_fusion, f32[2,64,40,64]{1,3,2,0:T(8,128)S(1)} %copy-done.3, f32[2,64,40,64]{1,3,2,0:T(8,128)S(1)} %copy.89, ...), kind=kOutput, calls=%fused_computation.36 | convolution fusion | flops 254279680 | bytes 7888896 | tf_op jit(solution)/shard_map/nhts,nshk->nthk/dot_general | solution.py:38
  366.8 11.1 %multiply_subtract_fusion = (f32[2,64,40,64]{1,3,2,0:T(8,128)}, f32[2,64,40,64]{1,3,2,0:T(8,128)}, bf16[2,64,40,64]{1,3,2,0:T(8,128)(2,1)}, bf16[2,64,40,64]{1,3,2,0:T(8,128)(2,1)}, f32[2,64,40]{1,2,0:T(8,128)}) fusion(f32[2,64,40,64]{1,3,2,0:T(8,128)S(1)} %copy-done.3, f32[2,64,40,64]{1,3,2,0:T(8,128)S(1)} %copy-done.5, f32[2,64,40,64]{1,3,2,0:T(8,128)} %fusion.9, ...), kind=kOutput, calls=%fused_computation.39 | convolution fusion | flops 258862080 | bytes 13203456 | tf_op jit(solution)/shard_map/nhst,nshk->nthk/dot_general | solution.py:38
  377.9 3.3 copy.131
  381.2 3.4 fusion.83
  384.6 3.3 copy.132
  387.8 4.9 subtract_subtract_fusion
  392.7 3.2 copy.133
  395.9 2.9 reshape.126
  406.6 3.5 mul.285
  412.6 9.8 %fusion.52 = f32[2,40,64,64]{3,2,1,0:T(8,128)} fusion(f32[2,64,40,64]{1,3,2,0:T(8,128)} %copy.93, f32[2,64,40,64]{1,3,2,0:T(8,128)S(1)} %copy.89, f32[2,40,64]{2,1,0:T(8,128)S(1)} %get-tuple-element.498, f32[2,64,40,64]{1,3,2,0:T(8,128)} %copy.91, f32[2,64,40,64]{1,3,2,0:T(8,128)S(1)} %copy-done.2), kind=kOutput, calls=%fused_computation.86 | convolution fusion | flops 253296640 | bytes 6574080 | tf_op jit(solution)/shard_map/nthk,nshk->nhts/dot_general | solution.py:38
  422.5 6.7 %fusion.23 = f32[2,40,64,64]{2,3,1,0:T(8,128)} fusion(f32[2,40,64,64]{2,3,1,0:T(8,128)S(1)} %copy-done.13, f32[40,64,64]{1,2,0:T(8,128)S(1)} %copy-done.18, f32[2,40,64]{2,1,0:T(8,128)S(1)} %copy-done.24, f32[2,64,40,64]{1,3,2,0:T(8,128)S(1)} %copy-done.4, f32[2,64,40,64]{1,3,2,0:T(8,128)S(1)} %copy.89, f32[2,40,64]{2,1,0:T(8,128)S(1)} %copy-done.22), kind=kOutput, calls=%fused_computation.63 | convolution fusion | flops 252968960 | bytes 5939200 | tf_op jit(solution)/shard_map/nthk,nhkv->nthv/dot_general | solution.py:38
  429.2 47.2 %all-reduce.9.cloned.1.call-done = (f32[2560,128]{0,1:T(8,128)}, f32[2560,128]{1,0:T(8,128)}) async-done(((f32[2560,128]{0,1:T(8,128)}, f32[2560,128]{1,0:T(8,128)}), (f32[2560,128]{0,1:T(8,128)}, f32[2560,128]{1,0:T(8,128)})) %all-reduce.9.cloned.1.call-update) | async-done | bytes 2621456 | tf_op jit(solution)/shard_map/psum | solution.py:14
  476.4 7.1 %fusion.7 = bf16[2,64,40,64]{3,1,2,0:T(8,128)(2,1)} fusion(f32[2,40,64,64]{2,3,1,0:T(8,128)} %fusion.23, f32[2,40,64,64]{3,2,1,0:T(8,128)} %fusion.52, f32[2,64,40]{1,2,0:T(8,128)S(1)} %copy-done.26, pred[64,64]{1,0:T(8,128)(4,1)S(1)} %iota_compare_fusion, bf16[2,64,40,64]{3,2,1,0:T(8,128)(2,1)} %reshape.125), kind=kOutput, calls=%fused_computation.30 | convolution fusion | flops 253624320 | bytes 3956736 | tf_op jit(solution)/shard_map/nhst,nshv->nthv/dot_general | solution.py:38
  483.5 7.1 %all-reduce.2 = (f32[2560]{0:T(1024)S(1)}, f32[2560]{0:T(1024)S(1)}) all-reduce(f32[2560]{0:T(1024)S(1)} %get-tuple-element.496, f32[2560]{0:T(1024)S(1)} %multiply_reduce_fusion.2), channel_id=1, replica_groups=mesh['seq'=16,'dp'=2] {'dp'}, use_global_device_ids=true, to_apply=%region_18.19 | all-reduce | flops 5120 | bytes 40960 | tf_op jit(solution)/shard_map/psum | solution.py:14
  490.6 60.5 %all-reduce = (f32[2560]{0:T(1024)S(1)}, f32[2560]{0:T(1024)S(1)}) all-reduce(f32[2560]{0:T(1024)S(1)} %get-tuple-element.479, f32[2560]{0:T(1024)S(1)} %get-tuple-element.480), channel_id=1, replica_groups=mesh['seq'=16,'dp'=2] {'seq'}, use_global_device_ids=true, to_apply=%region_19.20 | all-reduce | flops 5120 | bytes 40960 | tf_op jit(solution)/shard_map/psum | solution.py:14
  552.5 3.3 copy.128
  555.8 2.8 convert_element_type.122
  558.6 8.8 %fusion.22 = f32[2,40,64,64]{2,3,1,0:T(8,128)S(1)} fusion(f32[2,40,64,64]{2,3,1,0:T(8,128)} %get-tuple-element.325, f32[40,64,64]{1,2,0:T(8,128)} %copy.103, f32[2,40,64]{2,1,0:T(8,128)S(1)} %get-tuple-element.321, f32[2,64,40,64]{1,3,2,0:T(8,128)} %copy.91, f32[2,64,40,64]{1,3,2,0:T(8,128)S(1)} %copy.89, f32[2,64,40,64]{1,3,2,0:T(8,128)} %copy.90), kind=kOutput, calls=%fused_computation.62 | convolution fusion | flops 252968960 | bytes 7229440 | tf_op jit(solution)/shard_map/nthk,nhkv->nthv/dot_general | solution.py:38
  (141 shorter events, 81.8 us)
Async XLA Ops:
  7.2 2.4 copy-start
  7.2 164.0 %all-gather.7.cloned.1.call-start = ((), (), s32[]{:S(2)}) async-start(), calls=%async_computation | async-start | bytes 22282240 | tf_op jit(solution)/shard_map/all_gather | solution.py:25
  12.8 1.5 copy-start.14
  18.9 9.6 %copy-start.21 = (f32[2,40,64]{2,1,0:T(8,128)}, f32[2,40,64]{2,1,0:T(8,128)S(1)}, u32[]{:S(2)}) copy-start(f32[2,40,64]{2,1,0:T(8,128)S(1)} %get-tuple-element.499) | copy-start | bytes 61444
  53.6 228.2 %all-gather.9.cloned.1.call-start = ((), (), s32[]{:S(2)}) async-start(), calls=%async_computation.1 | async-start | bytes 22282240 | tf_op jit(solution)/shard_map/all_gather | solution.py:25
  105.3 371.0 %all-reduce.9.cloned.1.call-start = ((), (), s32[]{:S(2)}) async-start(), calls=%async_computation.3 | async-start | bytes 5242880 | tf_op jit(solution)/shard_map/psum | solution.py:14
  106.2 53.0 %copy-start.7 = (bf16[2,64,40,64]{3,2,1,0:T(8,128)(2,1)S(1)}, bf16[2,64,40,64]{3,2,1,0:T(8,128)(2,1)}, u32[]{:S(2)}) copy-start(bf16[2,64,40,64]{3,2,1,0:T(8,128)(2,1)} %reshape.124) | copy-start | bytes 1966084
  106.2 53.0 %copy-start.9 = (bf16[2,64,40,64]{3,2,1,0:T(8,128)(2,1)S(1)}, bf16[2,64,40,64]{3,2,1,0:T(8,128)(2,1)}, u32[]{:S(2)}) copy-start(bf16[2,64,40,64]{3,2,1,0:T(8,128)(2,1)} %reshape.125) | copy-start | bytes 1966084
  343.4 2.8 copy-start.23
  346.2 6.4 %copy-start.6 = (f32[2,40,64,64]{2,3,1,0:T(8,128)S(1)}, f32[2,40,64,64]{2,3,1,0:T(8,128)}, u32[]{:S(2)}) copy-start(f32[2,40,64,64]{2,3,1,0:T(8,128)} %get-tuple-element.781) | copy-start | bytes 3932164
  346.2 6.4 %copy-start.11 = (f32[2,40,64,64]{2,3,1,0:T(8,128)S(1)}, f32[2,40,64,64]{2,3,1,0:T(8,128)}, u32[]{:S(2)}) copy-start(f32[2,40,64,64]{2,3,1,0:T(8,128)} %get-tuple-element.325) | copy-start | bytes 3932164
  346.2 6.4 %copy-start.12 = (f32[2,40,64,64]{2,3,1,0:T(8,128)S(1)}, f32[2,40,64,64]{2,3,1,0:T(8,128)}, u32[]{:S(2)}) copy-start(f32[2,40,64,64]{2,3,1,0:T(8,128)} %get-tuple-element.330) | copy-start | bytes 3932164
  352.7 4.1 copy-start.10
  352.7 4.1 copy-start.17
  356.8 2.4 copy-start.1
  356.8 2.5 copy-start.3
  356.8 3.3 copy-start.16
  360.1 6.7 %copy-start.5 = (f32[2,64,40,64]{1,3,2,0:T(8,128)S(1)}, f32[2,64,40,64]{1,3,2,0:T(8,128)}, u32[]{:S(2)}) copy-start(f32[2,64,40,64]{1,3,2,0:T(8,128)} %copy.91) | copy-start | bytes 3932164
  360.1 6.7 %copy-start.22 = (f32[2,40,64]{2,1,0:T(8,128)S(1)}, f32[2,40,64]{2,1,0:T(8,128)}, u32[]{:S(2)}) copy-start(f32[2,40,64]{2,1,0:T(8,128)} %copy-done.21) | copy-start | bytes 61444
  360.1 6.7 %copy-start.25 = (f32[2,64,40]{1,2,0:T(8,128)S(1)}, f32[2,64,40]{1,2,0:T(8,128)}, u32[]{:S(2)}) copy-start(f32[2,64,40]{1,2,0:T(8,128)} %fusion.5) | copy-start | bytes 61444
  398.8 4.3 copy-start.20
  402.5 0.6 copy-start.28
  404.6 176.2 %all-reduce.7.cloned.1.call-start = ((), (), s32[]{:S(2)}) async-start(), calls=%async_computation.2 | async-start | bytes 5242880 | tf_op jit(solution)/shard_map/psum | solution.py:14
  410.1 2.5 copy-start.2
  412.6 9.8 %copy-start.4 = (f32[2,64,40,64]{1,3,2,0:T(8,128)S(1)}, f32[2,64,40,64]{1,3,2,0:T(8,128)}, u32[]{:S(2)}) copy-start(f32[2,64,40,64]{1,3,2,0:T(8,128)} %copy.93) | copy-start | bytes 3932164
  412.6 9.8 %copy-start.13 = (f32[2,40,64,64]{2,3,1,0:T(8,128)S(1)}, f32[2,40,64,64]{2,3,1,0:T(8,128)}, u32[]{:S(2)}) copy-start(f32[2,40,64,64]{2,3,1,0:T(8,128)} %get-tuple-element.330) | copy-start | bytes 3932164
  412.6 9.9 %copy-start.18 = (f32[40,64,64]{1,2,0:T(8,128)S(1)}, f32[40,64,64]{1,2,0:T(8,128)}, u32[]{:S(2)}) copy-start(f32[40,64,64]{1,2,0:T(8,128)} %copy.119) | copy-start | bytes 1966084
  412.6 9.9 %copy-start.24 = (f32[2,40,64]{2,1,0:T(8,128)S(1)}, f32[2,40,64]{2,1,0:T(8,128)}, u32[]{:S(2)}) copy-start(f32[2,40,64]{2,1,0:T(8,128)} %get-tuple-element.326) | copy-start | bytes 61444
  429.2 47.2 %copy-start.26 = (f32[2,64,40]{1,2,0:T(8,128)S(1)}, f32[2,64,40]{1,2,0:T(8,128)}, u32[]{:S(2)}) copy-start(f32[2,64,40]{1,2,0:T(8,128)} %get-tuple-element.495) | copy-start | bytes 61444
  558.6 8.8 %copy-start.8 = (bf16[2,64,40,64]{3,2,1,0:T(8,128)(2,1)S(1)}, bf16[2,64,40,64]{3,2,1,0:T(8,128)(2,1)}, u32[]{:S(2)}) copy-start(bf16[2,64,40,64]{3,2,1,0:T(8,128)(2,1)} %reshape.124) | copy-start | bytes 1966084
  558.6 8.8 %copy-start.15 = (f32[2,40,64,64]{3,2,1,0:T(8,128)S(1)}, f32[2,40,64,64]{3,2,1,0:T(8,128)}, u32[]{:S(2)}) copy-start(f32[2,40,64,64]{3,2,1,0:T(8,128)} %fusion.52) | copy-start | bytes 3932164
  572.3 3.6 copy-start.19
  575.9 2.5 copy-start.29
  580.8 2.3 copy-start.27
Sparse Core Ops, SparseCore 0:
  53.7 117.4 all-gather.6
  172.8 108.9 all-gather.8
  404.7 71.6 all-reduce.8
  479.9 100.8 all-reduce.6
